TPU v7x, 32 devices: a whole 2x2x4 slice. The times are simulated.
32 devices in a mesh: chain: 4 (over x, core), blk: 8 (over z, y).
Axes of the slice: x: 2, y: 2, z: 4, core: 2. Of those that a mesh axis runs over, the one named last changes fastest.
Arguments:
- schur: bfloat16 [8192, 2048], P(('chain', 'blk')), as said below
- coupling: bfloat16 [8192, 2048], P(('chain', 'blk')), may hold values from -0.0625 to 0.0625
- next_diag: float32 [8192, 2048], P(('chain', 'blk')), as said below
Outputs:
- factor: float32 [8192, 2048], P(('chain', 'blk'))
- next_schur: float32 [8192, 2048], P(('chain', 'blk'))
Inputs may be any that keep to these rules, and one draw needn't show every extreme that they name: `schur`: every slab's block is symmetric positive definite. `next_diag`: every slab's block is symmetric positive definite.
All inputs are finite; a program needn't handle non-finite values.
Results may differ from a plain program's by a relative error of at most 0.0034.
Values may be sent and summed in bfloat16 or wider, within the bound.
A program may use at most 128 MiB of HBM per device.

v0:
```python
import functools
import jax
import jax.numpy as jnp
from jax import lax
from jax.experimental import pallas as pl
from jax.experimental.pallas import tpu as pltpu
from jax.sharding import PartitionSpec as P

B = 128
BF = jnp.bfloat16
F32 = jnp.float32


def split(x):
    hi = x.astype(BF)
    return hi, (x - hi.astype(F32)).astype(BF)


def dot_t(a, b):
    return lax.dot_general(a, b, (((1,), (1,)), ((), ())), preferred_element_type=F32)


def eliminate(block):
    size = block.shape[0]
    count = size // 8
    sub = lax.broadcasted_iota(jnp.int32, (8, size), 0)
    lane = lax.broadcasted_iota(jnp.int32, (8, size), 1)
    rows = [block[8 * t : 8 * t + 8, :] for t in range(count)]
    inv = [jnp.where(lane == sub + 8 * t, 1.0, 0.0).astype(F32) for t in range(count)]
    group = 4

    def lane_of(x, k):
        return jnp.broadcast_to(x[:, k : k + 1], (8, size))

    def row_of(x, r):
        return jnp.broadcast_to(x[r : r + 1, :], (8, size))

    for k in range(0, size, group):
        s, r = divmod(k, 8)
        span = range(group)
        u = [row_of(rows[s], r + i) for i in span]
        n = [row_of(inv[s], r + i) for i in span]
        pivot = [[lane_of(u[i], k + j) if j >= i else None for j in span] for i in span]
        scale = [None] * group
        for i in span:
            scale[i] = lax.rsqrt(pivot[i][i])
            u[i] = u[i] * scale[i]
            n[i] = n[i] * scale[i]
            for j in range(i + 1, group):
                pivot[i][j] = pivot[i][j] * scale[i]
            for j in range(i + 1, group):
                u[j] = u[j] - pivot[i][j] * u[i]
                n[j] = n[j] - pivot[i][j] * n[i]
                for m in range(j, group):
                    pivot[j][m] = pivot[j][m] - pivot[i][j] * pivot[i][m]
        for t in range(s, count):
            if t == s and r + group == 8:
                new_a, new_n = rows[t], inv[t]
            else:
                c = [lane_of(rows[t], k + i) for i in span]
                new_a, new_n = rows[t], inv[t]
                for i in span:
                    x = c[i] * scale[i]
                    for j in range(i + 1, group):
                        c[j] = c[j] - x * pivot[i][j]
                    if t == s:
                        x = jnp.where(sub >= r + group, x, 0.0)
                    new_a = new_a - x * u[i]
                    new_n = new_n - x * n[i]
            if t == s:
                for i in span:
                    new_a = jnp.where(sub == r + i, u[i], new_a)
                    new_n = jnp.where(sub == r + i, n[i], new_n)
            rows[t], inv[t] = new_a, new_n
    return jnp.concatenate(rows, 0), jnp.concatenate(inv, 0)


def chunk_kernel(total, start, s_ref, c_ref, *refs):
    priors = refs[:-6]
    x_ref, f_ref, y_ref, work, left, right = refs[-6:]
    extra, width = c_ref.shape
    T = 2 * B
    me = lax.axis_index("blk")
    tail = pl.ds(total, extra)
    own = pl.ds(start, width)

    def tile(i):
        return pl.ds(pl.multiple_of(i * T, T), T)

    def over_rows(first, visit):
        def step(i, _):
            visit(tile(i))
            return 0

        lax.fori_loop(first, total // T, step, 0)
        visit(tail)

    def bring(rr, value):
        for prior in priors:
            hi, lo = prior[rr, :width], prior[rr, width:]
            own_hi, own_lo = prior[own, :width], prior[own, width:]
            value = value - (dot_t(hi, own_hi) + (dot_t(hi, own_lo) + dot_t(lo, own_hi)))
        work[rr, :] = value

    def load(i, _):
        bring(tile(i), s_ref[tile(i), :].astype(F32))
        return 0

    lax.fori_loop(start // T, total // T, load, 0)
    bring(tail, c_ref[...].astype(F32))
    tri = lax.broadcasted_iota(jnp.int32, (B, B), 0) >= lax.broadcasted_iota(jnp.int32, (B, B), 1)

    def panel(p, _):
        at = pl.multiple_of(p * B, B)
        here = pl.ds(pl.multiple_of(start + at, B), B)
        col = pl.ds(at, B)
        low_col = pl.ds(pl.multiple_of(width + at, B), B)
        slot = pl.ds(pl.multiple_of((p % 2) * 3 * B, 3 * B), 3 * B)
        upper, inv = eliminate(work[here, col])
        ih, il = split(inv)
        inv3 = jnp.concatenate([ih, il, ih], 1)
        first = start // T + p // 2

        def solve(rr):
            bh, bl = split(work[rr, col])
            x = dot_t(jnp.concatenate([bh, bh, bl], 1), inv3)
            work[rr, col] = x
            xh, xl = split(x)
            left[rr, slot] = jnp.concatenate([xh, xh, xl], 1)
            right[rr, slot] = jnp.concatenate([xh, xl, xh], 1)
            x_ref[rr, col] = xh
            x_ref[rr, low_col] = xl

        over_rows(first, solve)
        work[here, col] = jnp.where(tri, upper.T, 0.0)

        @pl.when(p % 2 == 0)
        def _():
            half = pl.ds(pl.multiple_of(at + B, B), B)
            b = right[pl.ds(pl.multiple_of(start + at + B, B), B), : 3 * B]

            def update(rr):
                work[rr, half] = work[rr, half] - dot_t(left[rr, : 3 * B], b)

            over_rows(first, update)

        @pl.when(p % 2 == 1)
        def _():
            def update_col(j, _):
                b = right[pl.ds(pl.multiple_of(start + j * T, T), T), :]

                def update(rr):
                    work[rr, tile(j)] = work[rr, tile(j)] - dot_t(left[rr, :], b)

                over_rows(start // T + j, update)
                return 0

            lax.fori_loop(p // 2 + 1, width // T, update_col, 0)

        return 0

    lax.fori_loop(0, width // B, panel, 0)
    row = me * extra + lax.broadcasted_iota(jnp.int32, (extra, width), 0)
    column = start + lax.broadcasted_iota(jnp.int32, (extra, width), 1)
    mine = work[pl.ds(pl.multiple_of(me * extra, extra), extra), :]
    f_ref[...] = jnp.where(row >= column, mine, 0.0)
    y_ref[...] = work[tail, :].astype(BF)


def chunk_call(start, s, c, priors):
    total, (extra, width) = s.shape[0], c.shape
    every = total + extra
    live = every - start
    vmem = pl.BlockSpec(memory_space=pltpu.VMEM)
    return pl.pallas_call(
        functools.partial(chunk_kernel, total, start),
        out_shape=(
            jax.ShapeDtypeStruct((every, 2 * width), BF),
            jax.ShapeDtypeStruct((extra, width), F32),
            jax.ShapeDtypeStruct((extra, width), BF),
        ),
        in_specs=[vmem] * (2 + len(priors)),
        out_specs=(vmem, vmem, vmem),
        scratch_shapes=[
            pltpu.VMEM((every, width), F32),
            pltpu.VMEM((every, 6 * B), BF),
            pltpu.VMEM((every, 6 * B), BF),
        ],
        compiler_params=pltpu.CompilerParams(vmem_limit_bytes=56 * 1024 * 1024),
        cost_estimate=pl.CostEstimate(flops=COST, bytes_accessed=8 * live * width, transcendentals=0),
        name="factor_chunk",
    )(s, c, *priors)


COST = 50000000000


def passed_along(value, axis, steps):
    count = lax.axis_size(axis)
    initial, last = (max(0, -steps), min(count, count - steps))
    return lax.ppermute(value, axis, [(source, source + steps) for source in range(initial, last)])


def local(schur, coupling, next_diag):
    total = schur.shape[1]
    width = max(total // 4, 2 * B)
    starts = range(0, total, width)
    early = lax.all_gather(schur[:, :width], "blk", axis=0, tiled=True)
    late = lax.all_gather(schur[:, width:], "blk", axis=0, tiled=True)
    wholes = [early] + [late[:, at - width : at] for at in starts[1:]]
    priors, factors = [], []
    fresh, waiting = next_diag, None
    for at, whole in zip(starts, wholes):
        held, rows, solved = chunk_call(at, whole, coupling[:, at : at + width], priors)
        priors.append(held)
        factors.append(rows)
        arrived = passed_along(solved, "chain", 1)
        priors, arrived = lax.optimization_barrier((priors, arrived))
        if waiting is not None:
            fresh = fresh - dot_t(*waiting)
            priors, fresh = lax.optimization_barrier((priors, fresh))
        waiting = (arrived, lax.all_gather(arrived, "blk", axis=0, tiled=True))
    fresh = fresh - dot_t(*waiting)
    return (jnp.concatenate(factors, axis=1), fresh)


def solution(mesh):
    placed = (P(("chain", "blk"), None),) * 3
    return jax.shard_map(
        local, mesh=mesh, in_specs=placed, out_specs=(P(("chain", "blk"), None),) * 2, check_vma=False
    )
```

profile of v0, /device:TPU:6, one launch (start us, length us, event | category | flops | bytes accessed | tf_op | source)
XLA Modules:
  0.0 378.9 jit_solution(802488639216754284)
XLA Ops:
  7.2 0.0 copy-start.9
  7.2 0.0 all-gather.7.cloned.1.call-start
  7.2 1.8 slice.27
  9.0 0.0 all-gather.7.cloned.1.call-update
  9.0 0.0 all-gather.9.cloned.1.call-start
  9.0 2.1 slice.29
  11.1 0.0 all-gather.9.cloned.1.call-update
  11.1 0.0 all-gather.11.cloned.1.call-start
  11.2 0.0 copy-done.9
  11.2 1.0 fusion.1
  12.2 47.3 %all-gather.7.cloned.1.call-done.s_ref = bf16[2048,512]{1,0:T(8,128)(2,1)} async-done(((bf16[256,512]{1,0:T(8,128)(2,1)}), bf16[2048,512]{1,0:T(8,128)(2,1)}) %all-gather.7.cloned.1.call-update) | async-done | bytes 2097168 | tf_op jit(solution)/shard_map/all_gather | solution.py:208
  59.5 41.8 %factor_chunk.4 = (bf16[2304,1024]{1,0:T(8,128)(2,1)}, f32[256,512]{1,0:T(8,128)}, bf16[256,512]{1,0:T(8,128)(2,1)}) custom-call(bf16[2048,512]{1,0:T(8,128)(2,1)} %all-gather.7.cloned.1.call-done.s_ref, bf16[256,512]{1,0:T(8,128)(2,1)} %get-tuple-element.63.c_ref), custom_call_target="tpu_custom_call" | custom-call | flops 49999998976 | bytes 9437184 | tf_op jit(solution)/shard_map/factor_chunk/pallas_call | solution.py:175
  101.3 1.9 collective-permute-start
  103.3 6.0 %collective-permute-done = bf16[256,512]{1,0:T(8,128)(2,1)S(1)} collective-permute-done((bf16[256,512]{1,0:T(8,128)(2,1)}, bf16[256,512]{1,0:T(8,128)(2,1)S(1)}, u32[]{:S(2)}, u32[]{:S(2)}) %collective-permute-start) | collective-permute-done | bytes 262176 | tf_op jit(solution)/shard_map/ppermute | solution.py:201
  109.2 0.7 copy-done.5
  109.9 0.0 all-gather.11.cloned.1.call-update
  110.0 0.0 all-gather.13.cloned.1.call-start
  110.0 49.5 %all-gather.9.cloned.1.call-done = bf16[2048,1536]{1,0:T(8,128)(2,1)} async-done(((bf16[256,1536]{1,0:T(8,128)(2,1)}), bf16[2048,1536]{1,0:T(8,128)(2,1)}) %all-gather.9.cloned.1.call-update) | async-done | bytes 6291472 | tf_op jit(solution)/shard_map/all_gather | solution.py:209
  159.5 5.7 %fusion = (bf16[2048,512]{1,0:T(8,128)(2,1)}, bf16[2048,512]{1,0:T(8,128)(2,1)}, bf16[2048,512]{1,0:T(8,128)(2,1)}) fusion(bf16[2048,1536]{1,0:T(8,128)(2,1)} %all-gather.9.cloned.1.call-done), kind=kLoop, calls=%fused_computation.5 | loop fusion | bytes 12582912 | tf_op jit(solution)/shard_map/slice | solution.py:210
  165.2 43.9 %factor_chunk.5 = (bf16[2304,1024]{1,0:T(8,128)(2,1)}, f32[256,512]{1,0:T(8,128)}, bf16[256,512]{1,0:T(8,128)(2,1)}) custom-call(bf16[2048,512]{1,0:T(8,128)(2,1)} %get-tuple-element.60.s_ref, bf16[256,512]{1,0:T(8,128)(2,1)} %get-tuple-element.62.c_ref, bf16[2304,1024]{1,0:T(8,128)(2,1)} %get-tuple-element.50.refs_0_), custom_call_target="tpu_custom_call" | custom-call | flops 49999998976 | bytes 7340032 | tf_op jit(solution)/shard_map/factor_chunk/pallas_call | solution.py:175
  209.1 1.9 collective-permute-start.1
  211.0 0.0 all-gather.11.cloned.1.call-done
  211.0 0.0 copy-done
  211.0 0.0 copy-done.6
  211.1 3.7 convolution_subtract_fusion.3
  214.7 2.3 collective-permute-done.1
  217.0 0.7 copy-done.3
  217.7 0.0 all-gather.13.cloned.1.call-update
  217.7 0.2 all-gather.15.cloned.1.call-start
  218.0 0.0 copy-start.4
  218.0 42.3 %factor_chunk.6 = (bf16[2304,1024]{1,0:T(8,128)(2,1)}, f32[256,512]{1,0:T(8,128)}, bf16[256,512]{1,0:T(8,128)(2,1)}) custom-call(bf16[2048,512]{1,0:T(8,128)(2,1)} %get-tuple-element.58.s_ref, bf16[256,512]{1,0:T(8,128)(2,1)} %get-tuple-element.61.c_ref, bf16[2304,1024]{1,0:T(8,128)(2,1)} %get-tuple-element.50.refs_0_, ...), custom_call_target="tpu_custom_call" | custom-call | flops 49999998976 | bytes 5242880 | tf_op jit(solution)/shard_map/factor_chunk/pallas_call | solution.py:175
  260.3 1.9 collective-permute-start.2
  262.2 6.0 %collective-permute-done.2 = bf16[256,512]{1,0:T(8,128)(2,1)S(1)} collective-permute-done((bf16[256,512]{1,0:T(8,128)(2,1)}, bf16[256,512]{1,0:T(8,128)(2,1)S(1)}, u32[]{:S(2)}, u32[]{:S(2)}) %collective-permute-start.2) | collective-permute-done | bytes 262176 | tf_op jit(solution)/shard_map/ppermute | solution.py:201
  268.2 0.7 copy-done.1
  268.9 0.0 all-gather.15.cloned.1.call-update
  268.9 0.0 all-gather.17.cloned.1.call-start
  269.0 0.0 all-gather.13.cloned.1.call-done
  269.0 3.0 convolution_subtract_fusion.2
  272.0 39.8 %factor_chunk.7 = (bf16[2304,1024]{1,0:T(8,128)(2,1)}, f32[256,512]{1,0:T(8,128)}, bf16[256,512]{1,0:T(8,128)(2,1)}) custom-call(bf16[2048,512]{1,0:T(8,128)(2,1)} %get-tuple-element.59.s_ref, bf16[256,512]{1,0:T(8,128)(2,1)} %get-tuple-element.64.c_ref, bf16[2304,1024]{1,0:T(8,128)(2,1)} %get-tuple-element.50.refs_0_, ...), custom_call_target="tpu_custom_call" | custom-call | flops 49999998976 | bytes 3145728 | tf_op jit(solution)/shard_map/factor_chunk/pallas_call | solution.py:175
  311.8 1.9 collective-permute-start.3
  313.7 6.0 %collective-permute-done.3 = bf16[256,512]{1,0:T(8,128)(2,1)S(1)} collective-permute-done((bf16[256,512]{1,0:T(8,128)(2,1)}, bf16[256,512]{1,0:T(8,128)(2,1)S(1)}, u32[]{:S(2)}, u32[]{:S(2)}) %collective-permute-start.3) | collective-permute-done | bytes 262176 | tf_op jit(solution)/shard_map/ppermute | solution.py:201
  319.6 0.7 copy-done.7
  320.3 0.0 all-gather.17.cloned.1.call-update
  320.4 2.9 pad_maximum_fusion
  323.3 0.0 copy-done.2
  323.3 3.7 convolution_subtract_fusion.1
  327.0 40.8 %all-gather.17.cloned.1.call-done = bf16[2048,512]{1,0:T(8,128)(2,1)} async-done(((bf16[256,512]{1,0:T(8,128)(2,1)}), bf16[2048,512]{1,0:T(8,128)(2,1)}) %all-gather.17.cloned.1.call-update) | async-done | bytes 2097168 | tf_op jit(solution)/shard_map/all_gather | solution.py:222
  367.8 4.3 %convolution_subtract_fusion = f32[256,2048]{1,0:T(8,128)} fusion(f32[256,2048]{1,0:T(8,128)} %convolution_subtract_fusion.1, bf16[256,512]{1,0:T(8,128)(2,1)S(1)} %copy-done.8, bf16[2048,512]{1,0:T(8,128)(2,1)} %all-gather.17.cloned.1.call-done), kind=kOutput, calls=%fused_computation | convolution fusion | flops 537395200 | bytes 6553600 | tf_op jit(solution)/shard_map/dot_general | solution.py:20
  (13 shorter events, 0.0 us)
Async XLA Ops:
  7.2 4.0 %copy-start.9 = (bf16[256,2048]{1,0:T(8,128)(2,1)S(1)}, bf16[256,2048]{1,0:T(8,128)(2,1)}, u32[]{:S(2)}) copy-start(bf16[256,2048]{1,0:T(8,128)(2,1)} %param.4) | copy-start | bytes 3145732
  7.2 52.3 %all-gather.7.cloned.1.call-start = ((), (), s32[]{:S(2)}) async-start(), calls=%async_computation | async-start | bytes 2359296 | tf_op jit(solution)/shard_map/all_gather | solution.py:208
  9.0 150.5 %all-gather.9.cloned.1.call-start = ((), (), s32[]{:S(2)}) async-start(), calls=%async_computation.1 | async-start | bytes 7077888 | tf_op jit(solution)/shard_map/all_gather | solution.py:209
  11.1 199.9 %all-gather.11.cloned.1.call-start = ((), (), s32[]{:S(2)}) async-start(), calls=%async_computation.2 | async-start | bytes 2359296 | tf_op jit(solution)/shard_map/all_gather | solution.py:222
  101.3 7.9 %collective-permute-start = (bf16[256,512]{1,0:T(8,128)(2,1)}, bf16[256,512]{1,0:T(8,128)(2,1)S(1)}, u32[]{:S(2)}, u32[]{:S(2)}) collective-permute-start(bf16[256,512]{1,0:T(8,128)(2,1)} %get-tuple-element.32), channel_id=1, source_target_pairs={{0,8},{8,16},{16,24},{1,9},{9,17},{17,25},{2,10},{10,18},{18,26},{... | collective-permute-start | bytes 786440 | tf_op jit(solution)/shard_map/ppermute | solution.py:201
  109.2 0.7 copy-start.5
  110.0 159.0 %all-gather.13.cloned.1.call-start = ((), (), s32[]{:S(2)}) async-start(), calls=%async_computation.3 | async-start | bytes 2359296 | tf_op jit(solution)/shard_map/all_gather | solution.py:222
  165.2 45.8 %copy-start = (f32[256,2048]{1,0:T(8,128)S(1)}, f32[256,2048]{1,0:T(8,128)}, u32[]{:S(2)}) copy-start(f32[256,2048]{1,0:T(8,128)} %param.5) | copy-start | bytes 6291460
  165.2 45.8 %copy-start.6 = (bf16[256,512]{1,0:T(8,128)(2,1)S(1)}, bf16[256,512]{1,0:T(8,128)(2,1)}, u32[]{:S(2)}) copy-start(bf16[256,512]{1,0:T(8,128)(2,1)} %copy-done.5) | copy-start | bytes 786436
  209.1 7.9 %collective-permute-start.1 = (bf16[256,512]{1,0:T(8,128)(2,1)}, bf16[256,512]{1,0:T(8,128)(2,1)S(1)}, u32[]{:S(2)}, u32[]{:S(2)}) collective-permute-start(bf16[256,512]{1,0:T(8,128)(2,1)} %get-tuple-element.36), channel_id=1, source_target_pairs={{0,8},{8,16},{16,24},{1,9},{9,17},{17,25},{2,10},{10,18},{18,26},{... | collective-permute-start | bytes 786440 | tf_op jit(solution)/shard_map/ppermute | solution.py:201
  217.0 0.7 copy-start.3
  217.7 105.6 %all-gather.15.cloned.1.call-start = ((), (), s32[]{:S(2)}) async-start(), calls=%async_computation.4 | async-start | bytes 2359296 | tf_op jit(solution)/shard_map/all_gather | solution.py:222
  218.0 51.0 %copy-start.4 = (bf16[256,512]{1,0:T(8,128)(2,1)S(1)}, bf16[256,512]{1,0:T(8,128)(2,1)}, u32[]{:S(2)}) copy-start(bf16[256,512]{1,0:T(8,128)(2,1)} %copy-done.3) | copy-start | bytes 786436
  260.3 7.9 %collective-permute-start.2 = (bf16[256,512]{1,0:T(8,128)(2,1)}, bf16[256,512]{1,0:T(8,128)(2,1)S(1)}, u32[]{:S(2)}, u32[]{:S(2)}) collective-permute-start(bf16[256,512]{1,0:T(8,128)(2,1)} %get-tuple-element.44), channel_id=1, source_target_pairs={{0,8},{8,16},{16,24},{1,9},{9,17},{17,25},{2,10},{10,18},{18,26},{... | collective-permute-start | bytes 786440 | tf_op jit(solution)/shard_map/ppermute | solution.py:201
  268.2 0.7 copy-start.1
  268.9 98.9 %all-gather.17.cloned.1.call-start = ((), (), s32[]{:S(2)}) async-start(), calls=%async_computation.5 | async-start | bytes 2359296 | tf_op jit(solution)/shard_map/all_gather | solution.py:222
  272.0 48.4 %copy-start.10 = (f32[256,512]{1,0:T(8,128)S(1)}, f32[256,512]{1,0:T(8,128)}, u32[]{:S(2)}) copy-start(f32[256,512]{1,0:T(8,128)} %get-tuple-element.30) | copy-start | bytes 1572868
  311.8 7.9 %collective-permute-start.3 = (bf16[256,512]{1,0:T(8,128)(2,1)}, bf16[256,512]{1,0:T(8,128)(2,1)S(1)}, u32[]{:S(2)}, u32[]{:S(2)}) collective-permute-start(bf16[256,512]{1,0:T(8,128)(2,1)} %get-tuple-element.56), channel_id=1, source_target_pairs={{0,8},{8,16},{16,24},{1,9},{9,17},{17,25},{2,10},{10,18},{18,26},{... | collective-permute-start | bytes 786440 | tf_op jit(solution)/shard_map/ppermute | solution.py:201
  319.6 0.7 copy-start.7
  320.4 2.9 copy-start.2
  323.3 44.5 %copy-start.8 = (bf16[256,512]{1,0:T(8,128)(2,1)S(1)}, bf16[256,512]{1,0:T(8,128)(2,1)}, u32[]{:S(2)}) copy-start(bf16[256,512]{1,0:T(8,128)(2,1)} %copy-done.7) | copy-start | bytes 786436
Sparse Core Ops, SparseCore 0:
  10.1 49.3 all-gather.6
  62.2 97.2 all-gather.8
  161.6 47.4 all-gather.10
  217.8 47.3 all-gather.12
  269.0 47.4 all-gather.14
  320.5 47.2 all-gather.16
where the time goes:
time: 382 us; the launch traced here: 379 us
  Pallas kernels  168 us (44%)
  waiting for transfers between devices  158 us (41%)
  matrix products  14.6 us (4%)
  between operations  14.2 us (4%)
  local copies, waits for them, and re-layouts  13.4 us (4%)
  starting transfers between devices  8.06 us (2%)
    pallas_call x4, Pallas kernels, chunk_call(): pl.pallas_call(functools.partial(chunk_kernel, total, start), out_shape=(...  168 us
    all_gather x1, waiting for transfers between devices, local(): late = lax.all_gather(schur[:, width:], 'blk', axis=0, tiled=True)  49.5 us
    all_gather x1, waiting for transfers between devices, local(): early = lax.all_gather(schur[:, :width], 'blk', axis=0, tiled=True)  47.3 us
    all_gather x4, waiting for transfers between devices, local(): waiting = (arrived, lax.all_gather(arrived, 'blk', axis=0, tiled=True))  40.8 us
    ppermute x4, waiting for transfers between devices, passed_along(): lax.ppermute(value, axis, [(source, source + steps) for source in range(i...  20.2 us
    dot_general x4, matrix products, dot_t(): lax.dot_general(a, b, (((1,), (1,)), ((), ())), preferred_element_type=F32)  14.6 us
  transfers between devices with their start and end apart: 10, of which 7 were waited for; matrix products, arithmetic and copies ran while one was open for 6% of the time, Pallas kernels for 44%

commit v1 on v0

v1 whole, which is shorter than its diff:
```python
import functools
import jax
import jax.numpy as jnp
from jax import lax
from jax.experimental import pallas as pl
from jax.experimental.pallas import tpu as pltpu
from jax.sharding import PartitionSpec as P

B = 128
T = 2 * B
BF = jnp.bfloat16
F32 = jnp.float32
MESH = pl.DeviceIdType.MESH


def split(x):
    hi = x.astype(BF)
    return hi, (x - hi.astype(F32)).astype(BF)


def dot_t(a, b):
    return lax.dot_general(a, b, (((1,), (1,)), ((), ())), preferred_element_type=F32)


def pair(x):
    return jnp.concatenate(split(x), 1)


def product_t(a, b):
    half = a.shape[1] // 2
    return dot_t(jnp.concatenate([a[:, :half], a], 1), jnp.concatenate([b, b[:, :half]], 1))


def product(a, b):
    ah, al = split(a)
    bh, bl = split(b)
    return jnp.dot(
        jnp.concatenate([ah, ah, al], 1), jnp.concatenate([bh, bl, bh], 0), preferred_element_type=F32
    )


def invert(block):
    size = block.shape[0]
    group = 8
    count = size // group
    sub = lax.broadcasted_iota(jnp.int32, (group, size), 0)
    lane = lax.broadcasted_iota(jnp.int32, (group, size), 1)
    rows = [block[group * t : group * t + group, :] for t in range(count)]
    span = range(group)

    def lane_of(x, k):
        return jnp.broadcast_to(x[:, k : k + 1], (group, size))

    def row_of(x, r):
        return jnp.broadcast_to(x[r : r + 1, :], (group, size))

    cols = [lane_of(rows[0], j) for j in span]
    for s in range(count):
        k = group * s
        more = s + 1 < count
        window = (lane >= k) & (lane < k + group)
        c = [[lane_of(rows[t], k + i) for i in span] for t in range(s + 1, count)]
        if more:
            ahead = [lane_of(rows[s + 1], k + group + j) for j in span]
            x = list(c[0])
        pivot = [[row_of(cols[j], i) if j >= i else None for j in span] for i in span]
        base = jnp.where(window, jnp.where(lane - k == sub, 1.0, 0.0), rows[s])
        u = [row_of(base, i) for i in span]
        scale = [None] * group
        for i in span:
            scale[i] = lax.rsqrt(pivot[i][i])
            u[i] = u[i] * scale[i]
            for j in range(i + 1, group):
                pivot[i][j] = pivot[i][j] * scale[i]
            if more:
                x[i] = x[i] * scale[i]
            for j in range(i + 1, group):
                u[j] = u[j] - pivot[i][j] * u[i]
                if more:
                    x[j] = x[j] - pivot[i][j] * x[i]
                for m in range(j, group):
                    pivot[j][m] = pivot[j][m] - pivot[i][j] * pivot[i][m]
            if more:
                for j in span:
                    ahead[j] = ahead[j] - x[i] * row_of(x[i], j)
        out = u[0]
        for i in range(1, group):
            out = jnp.where(sub == i, u[i], out)
        rows[s] = jnp.where(lane - k <= sub, out, 0.0)
        w = list(u)
        for i in reversed(span):
            w[i] = w[i] * scale[i]
            for j in range(i):
                w[j] = w[j] - pivot[j][i] * w[i]
        for t in range(s + 1, count):
            new = jnp.where(window, 0.0, rows[t])
            for i in reversed(span):
                new = new - c[t - s - 1][i] * w[i]
            rows[t] = new
        if more:
            cols = ahead
    return jnp.concatenate(rows, 0)


def kernel(
    ny, s_ref, c_ref, d_ref, f_ref, o_ref,
    gathered, low, work, inverse, solved, others,
    s_recv, s_send_z, s_send_y, c_recv, c_send, y_recv, y_send_z, y_send_y,
):
    extra, total = s_ref.shape
    count = total // T
    per = T // extra
    n = total // extra
    nz = n // ny
    me = lax.axis_index("blk")
    z, y = me // ny, me % ny
    link, links = lax.axis_index("chain"), lax.axis_size("chain")
    mine = pl.ds(pl.multiple_of(me * extra, extra), extra)
    tail = pl.ds(total, extra)
    z_peers = [(lax.rem(z + i, nz) * ny + y) for i in range(1, nz)]
    y_peers = [(z * ny + lax.rem(y + i, ny)) for i in range(1, ny)]
    has_next, has_prior = link + 1 < links, link > 0

    def tile(i):
        return pl.ds(pl.multiple_of(i * T, T), T)

    def rows_of(b):
        return pl.ds(pl.multiple_of(b * extra, extra), extra)

    def remote(src, dst, send, recv, **to):
        return pltpu.make_async_remote_copy(
            src_ref=src, dst_ref=dst, send_sem=send, recv_sem=recv, device_id=to, device_id_type=MESH
        )

    barrier = pltpu.get_barrier_semaphore()
    for peer in z_peers + y_peers:
        pl.semaphore_signal(barrier, inc=1, device_id={"blk": peer}, device_id_type=MESH)
    for has, step in ((has_next, 1), (has_prior, -1)):

        @pl.when(has)
        def _():
            pl.semaphore_signal(barrier, inc=1, device_id={"chain": link + step}, device_id_type=MESH)

    pl.semaphore_wait(barrier, nz + ny - 2 + has_next.astype(jnp.int32) + has_prior.astype(jnp.int32))

    def s_own(k):
        src = s_ref.at[:, tile(k)]
        dst = gathered.at[k, mine, :]
        out = []
        for i, peer in enumerate(z_peers):
            out.append(remote(src, dst, s_send_z.at[k, i], s_recv.at[k, me], blk=peer))
        for i, peer in enumerate(y_peers):
            out.append(remote(src, dst, s_send_y.at[k, z, i], s_recv.at[k, me], blk=peer))
        return out

    def s_from(k, b):
        at = gathered.at[k, rows_of(b), :]
        return remote(at, at, s_send_z.at[k, 0], s_recv.at[k, b], blk=z_peers[0])

    def s_on(k, zz):
        at = gathered.at[k, rows_of(zz * ny + y), :]
        return [
            remote(at, at, s_send_y.at[k, zz, i], s_recv.at[k, zz * ny + y], blk=peer)
            for i, peer in enumerate(y_peers)
        ]

    def s_has(k, b):
        return (b * extra) // T >= k

    def s_forward(k, zz):
        @pl.when((zz != z) & s_has(k, zz * ny + y))
        def _():
            s_from(k, zz * ny + y).wait_recv()
            for copy in s_on(k, zz):
                copy.start()

    def s_wait(k, i):
        for q in range(per):
            b = i * per + q

            @pl.when(b % ny != y)
            def _():
                s_from(k, b).wait_recv()

    def over_z(first, visit):
        def step(zz, _):
            visit(zz)
            return 0

        lax.fori_loop(first, nz, step, 0)

    def over(first, last, visit):
        def step(k, _):
            visit(k)
            return 0

        lax.fori_loop(first, last, step, 0)

    def start_own(k):
        @pl.when(s_has(k, me))
        def _():
            for copy in s_own(k):
                copy.start()

    over(0, count, start_own)

    def y_hop(k):
        at = others.at[k, mine, :]
        return remote(solved.at[k], at, c_send.at[k], c_recv.at[k], chain=lax.min(link + 1, links - 1))

    def y_own(k):
        at = others.at[k, mine, :]
        out = []
        for i, peer in enumerate(z_peers):
            out.append(remote(at, at, y_send_z.at[k, i], y_recv.at[k, me], blk=peer))
        for i, peer in enumerate(y_peers):
            out.append(remote(at, at, y_send_y.at[k, z, i], y_recv.at[k, me], blk=peer))
        return out

    def y_from(k, b):
        at = others.at[k, rows_of(b), :]
        return remote(at, at, y_send_z.at[k, 0], y_recv.at[k, b], blk=z_peers[0])

    def y_on(k, zz):
        at = others.at[k, rows_of(zz * ny + y), :]
        return [
            remote(at, at, y_send_y.at[k, zz, i], y_recv.at[k, zz * ny + y], blk=peer)
            for i, peer in enumerate(y_peers)
        ]

    def y_spread(k):
        y_hop(k).wait_recv()
        for copy in y_own(k):
            copy.start()

    def y_forward(k):
        def visit(zz):
            @pl.when(zz != z)
            def _():
                y_from(k, zz * ny + y).wait_recv()
                for copy in y_on(k, zz):
                    copy.start()

        over_z(0, visit)

    def y_use(k):
        def arrive(b):
            @pl.when(b % ny != y)
            def _():
                y_from(k, b).wait_recv()

        over(0, n, arrive)
        own = others[k, mine, :]

        def visit(j):
            o_ref[:, tile(j)] = o_ref[:, tile(j)] - dot_t(own, others[k, tile(j), :])

        over(0, count, visit)

    def y_stage(k):
        for lag, act in ((1, y_spread), (2, y_forward), (3, y_use)):

            @pl.when(has_prior & (k >= lag) & (k - lag < count))
            def _():
                act(k - lag)

    def keep(k):
        gathered[k, mine, :] = s_ref[:, tile(k)]
        o_ref[:, tile(k)] = d_ref[:, tile(k)]

    over(0, count, keep)
    s_forward(0, 0)

    def bring(k, rr, value):
        work[rr, :] = value.astype(F32)

        def step(j):
            work[rr, :] = work[rr, :] - product_t(low[j, rr, :], low[j, tile(k), :])

        over(0, k, step)

    def solve(k, rr):
        x = product_t(pair(work[rr, :]), inverse[...])
        low[k, rr, :] = pair(x)
        return x

    def chunk(k):
        s_wait(k, k)
        bring(k, tile(k), gathered[k, tile(k), :])
        at = pl.multiple_of(k * T, T)
        first, second = pl.ds(at, B), pl.ds(pl.multiple_of(at + B, B), B)
        n1 = invert(work[first, :B])
        x21 = product_t(pair(work[second, :B]), pair(n1))
        p21 = pair(x21)
        n2 = invert(work[second, B:] - product_t(p21, p21))
        m21 = product(n2, product(x21, n1))
        inverse[:B, :] = pair(jnp.concatenate([n1, jnp.zeros((B, B), F32)], 1))
        inverse[B:, :] = pair(jnp.concatenate([-m21, n2], 1))

        @pl.when(k == 0)
        def _():
            over_z(1, lambda zz: s_forward(0, zz))

        bring(k, tail, c_ref[:, tile(k)])
        solved[k] = solve(k, tail).astype(BF)
        solve(k, tile(k))

        def rest(i):
            s_wait(k, i)
            bring(k, tile(i), gathered[k, tile(i), :])
            solve(k, tile(i))

        over(k + 1, count, rest)

        @pl.when(has_next)
        def _():
            y_hop(k).start()

        row = me * extra + lax.broadcasted_iota(jnp.int32, (extra, T), 0)
        column = k * T + lax.broadcasted_iota(jnp.int32, (extra, T), 1)

        @pl.when(s_has(k, me))
        def _():
            both = low[k, mine, :]
            f_ref[:, tile(k)] = jnp.where(row >= column, both[:, :T].astype(F32) + both[:, T:].astype(F32), 0.0)

        @pl.when(jnp.logical_not(s_has(k, me)))
        def _():
            f_ref[:, tile(k)] = jnp.zeros((extra, T), F32)

        @pl.when(k + 1 < count)
        def _():
            over_z(0, lambda zz: s_forward(k + 1, zz))

        y_stage(k)

    over(0, count, chunk)
    over(count, count + 3, y_stage)

    def settle(k):
        @pl.when(s_has(k, me))
        def _():
            for copy in s_own(k):
                copy.wait_send()

        def visit(zz):
            @pl.when((zz != z) & s_has(k, zz * ny + y))
            def _():
                for copy in s_on(k, zz):
                    copy.wait_send()

            @pl.when((zz != z) & has_prior)
            def _():
                for copy in y_on(k, zz):
                    copy.wait_send()

        over_z(0, visit)

        @pl.when(has_prior)
        def _():
            for copy in y_own(k):
                copy.wait_send()

        @pl.when(has_next)
        def _():
            y_hop(k).wait_send()

    over(0, count, settle)


def local(schur, coupling, next_diag):
    extra, total = schur.shape
    n = lax.axis_size("blk")
    ny = 1 << ((n.bit_length() - 1) // 2)
    nz = n // ny
    count = total // T
    vmem = pl.BlockSpec(memory_space=pltpu.VMEM)
    sems = pltpu.SemaphoreType.DMA
    return pl.pallas_call(
        functools.partial(kernel, ny),
        out_shape=(jax.ShapeDtypeStruct((extra, total), F32),) * 2,
        in_specs=[vmem] * 3,
        out_specs=(vmem, vmem),
        scratch_shapes=[
            pltpu.VMEM((count, total, T), BF),
            pltpu.VMEM((count, total + extra, 2 * T), BF),
            pltpu.VMEM((total + extra, T), F32),
            pltpu.VMEM((T, 2 * T), BF),
            pltpu.VMEM((count, extra, T), BF),
            pltpu.VMEM((count, total, T), BF),
            sems((count, n)),
            sems((count, nz - 1)),
            sems((count, nz, max(ny - 1, 1))),
            sems((count,)),
            sems((count,)),
            sems((count, n)),
            sems((count, nz - 1)),
            sems((count, nz, max(ny - 1, 1))),
        ],
        compiler_params=pltpu.CompilerParams(
            vmem_limit_bytes=60 * 1024 * 1024, collective_id=0, has_side_effects=True
        ),
        name="slab_step",
    )(schur, coupling, next_diag)


def solution(mesh):
    placed = (P(("chain", "blk"), None),) * 3
    return jax.shard_map(
        local, mesh=mesh, in_specs=placed, out_specs=(P(("chain", "blk"), None),) * 2, check_vma=False
    )
```

time: 382 us -> 232 us (0.61)
  waiting for transfers between devices: 158 us -> 0 us
  Pallas kernels: 168 us -> 225 us
  matrix products: 14.6 us -> 0 us
  between operations: 14.2 us -> 0.65 us
  local copies, waits for them, and re-layouts: 13.4 us -> 4.61 us
  starting transfers between devices: 8.06 us -> 0 us
    all_gather x6 -> x0, waiting for transfers between devices: 138 us -> none  [the longest x1 49.5 us: local(): late = lax.all_gather(schur[:, width:], 'blk', axis=0, tiled=True)]
    pallas_call x4 -> x1, Pallas kernels: 168 us -> 225 us  [local(): pl.pallas_call(functools.partial(kernel, ny), out_shape=(jax.ShapeDtypeSt...]
    ppermute x4 -> x0, waiting for transfers between devices: 20.2 us -> none  [passed_along(): lax.ppermute(value, axis, [(source, source + steps) for source in range(i...]
    dot_general x4 -> x0, matrix products: 14.6 us -> none  [dot_t(): lax.dot_general(a, b, (((1,), (1,)), ((), ())), preferred_element_type=F32)]
    slice x4 -> x0, local copies, waits for them, and re-layouts: 10.5 us -> none  [the longest x1 5.71 us: local(): wholes = [early] + [late[:, at - width:at] for at in starts[1:]]]
    ppermute x4 -> x0, starting transfers between devices: 7.63 us -> none  [passed_along(): lax.ppermute(value, axis, [(source, source + steps) for source in range(i...]
  transfers between devices with their start and end apart: 10 -> 0, of which waited for: 7 -> 0; matrix products, arithmetic and copies ran while one was open for 6% -> 0% of each run, Pallas kernels for 44% -> 0%
where the time goes in v1:
time: 232 us; the launch traced here: 230 us
  Pallas kernels  225 us (97%)
  local copies, waits for them, and re-layouts  4.61 us (2%)
    pallas_call x1, Pallas kernels, local(): pl.pallas_call(functools.partial(kernel, ny), out_shape=(jax.ShapeDtypeSt...  225 us

profile of v1, /device:TPU:6, one launch (start us, length us, event | category | flops | bytes accessed | tf_op | source)
XLA Modules:
  0.0 230.0 jit_solution(15604527807314277976)
XLA Ops:
  0.6 224.7 %slab_step.1 = (f32[256,2048]{1,0:T(8,128)}, f32[256,2048]{1,0:T(8,128)}) custom-call(bf16[256,2048]{1,0:T(8,128)(2,1)} %s_ref.1, bf16[256,2048]{1,0:T(8,128)(2,1)} %c_ref.1, f32[256,2048]{1,0:T(8,128)} %d_ref.1), custom_call_target="tpu_custom_call" | custom-call | tf_op jit(solution)/shard_map/slab_step/pallas_call | solution.py:379
  225.4 0.0 copy-start
  225.4 3.3 %copy.7 = f32[256,2048]{1,0:T(8,128)} copy(f32[256,2048]{1,0:T(8,128)} %get-tuple-element.4) | data formatting | bytes 4194304
  228.6 0.0 copy-done
  228.6 1.3 copy.8
Async XLA Ops:
  225.4 3.3 %copy-start = (f32[256,2048]{1,0:T(8,128)S(1)}, f32[256,2048]{1,0:T(8,128)}, u32[]{:S(2)}) copy-start(f32[256,2048]{1,0:T(8,128)} %get-tuple-element.5) | copy-start | bytes 6291460

commit v2 on v1

--- a/solution.py
+++ b/solution.py
@@ -8,6 +8,8 @@
 
 B = 128
 T = 2 * B
+LAG = 2
+USE = 2
 BF = jnp.bfloat16
 F32 = jnp.float32
 MESH = pl.DeviceIdType.MESH
@@ -39,7 +41,7 @@
     )
 
 
-def invert(block):
+def invert(block, beside=()):
     size = block.shape[0]
     group = 8
     count = size // group
@@ -97,6 +99,8 @@
             for i in reversed(span):
                 new = new - c[t - s - 1][i] * w[i]
             rows[t] = new
+        if s % 2 and s // 2 < len(beside):
+            beside[s // 2]()
         if more:
             cols = ahead
     return jnp.concatenate(rows, 0)
@@ -105,7 +109,7 @@
 def kernel(
     ny, s_ref, c_ref, d_ref, f_ref, o_ref,
     gathered, low, work, inverse, solved, others,
-    s_recv, s_send_z, s_send_y, c_recv, c_send, y_recv, y_send_z, y_send_y,
+    s_recv, s_send_z, s_send_y, c_recv, c_send, y_recv, y_send_z, y_send_y, s_direct, y_direct,
 ):
     extra, total = s_ref.shape
     count = total // T
@@ -117,7 +121,9 @@
     link, links = lax.axis_index("chain"), lax.axis_size("chain")
     mine = pl.ds(pl.multiple_of(me * extra, extra), extra)
     tail = pl.ds(total, extra)
-    z_peers = [(lax.rem(z + i, nz) * ny + y) for i in range(1, nz)]
+    up, down = lax.min(z + 1, nz - 1) * ny + y, lax.max(z - 1, 0) * ny + y
+    has_up, has_down = z + 1 < nz, z > 0
+    z_peers = [lax.rem(z + i, nz) * ny + y for i in range(1, nz)]
     y_peers = [(z * ny + lax.rem(y + i, ny)) for i in range(1, ny)]
     has_next, has_prior = link + 1 < links, link > 0
 
@@ -133,46 +139,80 @@
         )
 
     barrier = pltpu.get_barrier_semaphore()
+    greeted = jnp.int32(nz + ny - 2)
     for peer in z_peers + y_peers:
         pl.semaphore_signal(barrier, inc=1, device_id={"blk": peer}, device_id_type=MESH)
-    for has, step in ((has_next, 1), (has_prior, -1)):
+    for has, to in (
+        (has_next, {"chain": link + 1}),
+        (has_prior, {"chain": link - 1}),
+    ):
+        greeted = greeted + has.astype(jnp.int32)
 
         @pl.when(has)
         def _():
-            pl.semaphore_signal(barrier, inc=1, device_id={"chain": link + step}, device_id_type=MESH)
-
-    pl.semaphore_wait(barrier, nz + ny - 2 + has_next.astype(jnp.int32) + has_prior.astype(jnp.int32))
-
-    def s_own(k):
-        src = s_ref.at[:, tile(k)]
+            pl.semaphore_signal(barrier, inc=1, device_id=to, device_id_type=MESH)
+
+    pl.semaphore_wait(barrier, greeted)
+
+    def along_z(zz):
+        return ((zz <= z) & has_up, up, 0), ((zz >= z) & has_down, down, 1)
+
+    def passing(src, dst, k, zz, send_z, send_y, recv, act, straight, direct):
+        at = recv.at[k, zz * ny + y]
+
+        @pl.when(straight & (zz == z))
+        def _():
+            for i, peer in enumerate(z_peers):
+                act(remote(src, dst, direct.at[lax.rem(k, 2), i], at, blk=peer))
+
+        for has, peer, way in along_z(zz):
+
+            @pl.when(has & jnp.logical_not(straight))
+            def _():
+                act(remote(src, dst, send_z.at[k, zz, way], at, blk=peer))
+
+        for i, peer in enumerate(y_peers):
+            act(remote(src, dst, send_y.at[k, zz, i], at, blk=peer))
+
+    def begin(copy):
+        copy.start()
+
+    def end(copy):
+        copy.wait_send()
+
+    def s_pass(k, zz, act):
+        at = gathered.at[k, rows_of(zz * ny + y), :]
+        passing(at, at, k, zz, s_send_z, s_send_y, s_recv, act, k < 2, s_direct)
+
+    def s_own(k, act):
         dst = gathered.at[k, mine, :]
-        out = []
-        for i, peer in enumerate(z_peers):
-            out.append(remote(src, dst, s_send_z.at[k, i], s_recv.at[k, me], blk=peer))
-        for i, peer in enumerate(y_peers):
-            out.append(remote(src, dst, s_send_y.at[k, z, i], s_recv.at[k, me], blk=peer))
-        return out
+        passing(s_ref.at[:, tile(k)], dst, k, z, s_send_z, s_send_y, s_recv, act, k < 2, s_direct)
 
     def s_from(k, b):
         at = gathered.at[k, rows_of(b), :]
-        return remote(at, at, s_send_z.at[k, 0], s_recv.at[k, b], blk=z_peers[0])
-
-    def s_on(k, zz):
-        at = gathered.at[k, rows_of(zz * ny + y), :]
-        return [
-            remote(at, at, s_send_y.at[k, zz, i], s_recv.at[k, zz * ny + y], blk=peer)
-            for i, peer in enumerate(y_peers)
-        ]
+        return remote(at, at, s_send_z.at[k, 0, 0], s_recv.at[k, b], blk=up)
 
     def s_has(k, b):
         return (b * extra) // T >= k
 
-    def s_forward(k, zz):
-        @pl.when((zz != z) & s_has(k, zz * ny + y))
-        def _():
-            s_from(k, zz * ny + y).wait_recv()
-            for copy in s_on(k, zz):
-                copy.start()
+    def both_ways(d, visit):
+        for zz in (z - d, z + d):
+
+            @pl.when((zz >= 0) & (zz < nz))
+            def _():
+                visit(zz)
+
+    def first(k, b):
+        return (k == 0) & (b < per)
+
+    def s_forward(k, d):
+        def visit(zz):
+            @pl.when(s_has(k, zz * ny + y) & jnp.logical_not(first(k, zz * ny + y)))
+            def _():
+                s_from(k, zz * ny + y).wait_recv()
+                s_pass(k, zz, begin)
+
+        both_ways(d, visit)
 
     def s_wait(k, i):
         for q in range(per):
@@ -181,13 +221,6 @@
             @pl.when(b % ny != y)
             def _():
                 s_from(k, b).wait_recv()
-
-    def over_z(first, visit):
-        def step(zz, _):
-            visit(zz)
-            return 0
-
-        lax.fori_loop(first, nz, step, 0)
 
     def over(first, last, visit):
         def step(k, _):
@@ -197,51 +230,35 @@
         lax.fori_loop(first, last, step, 0)
 
     def start_own(k):
-        @pl.when(s_has(k, me))
-        def _():
-            for copy in s_own(k):
-                copy.start()
-
-    over(0, count, start_own)
+        @pl.when((k < count) & s_has(k, me))
+        def _():
+            s_own(k, begin)
+
+    for k in range(3):
+        start_own(k)
 
     def y_hop(k):
         at = others.at[k, mine, :]
         return remote(solved.at[k], at, c_send.at[k], c_recv.at[k], chain=lax.min(link + 1, links - 1))
 
-    def y_own(k):
-        at = others.at[k, mine, :]
-        out = []
-        for i, peer in enumerate(z_peers):
-            out.append(remote(at, at, y_send_z.at[k, i], y_recv.at[k, me], blk=peer))
-        for i, peer in enumerate(y_peers):
-            out.append(remote(at, at, y_send_y.at[k, z, i], y_recv.at[k, me], blk=peer))
-        return out
+    def y_pass(k, zz, act):
+        at = others.at[k, rows_of(zz * ny + y), :]
+        passing(at, at, k, zz, y_send_z, y_send_y, y_recv, act, k == count - 1, y_direct)
 
     def y_from(k, b):
         at = others.at[k, rows_of(b), :]
-        return remote(at, at, y_send_z.at[k, 0], y_recv.at[k, b], blk=z_peers[0])
-
-    def y_on(k, zz):
-        at = others.at[k, rows_of(zz * ny + y), :]
-        return [
-            remote(at, at, y_send_y.at[k, zz, i], y_recv.at[k, zz * ny + y], blk=peer)
-            for i, peer in enumerate(y_peers)
-        ]
+        return remote(at, at, y_send_z.at[k, 0, 0], y_recv.at[k, b], blk=up)
 
     def y_spread(k):
         y_hop(k).wait_recv()
-        for copy in y_own(k):
-            copy.start()
-
-    def y_forward(k):
+        y_pass(k, z, begin)
+
+    def y_forward(k, d):
         def visit(zz):
-            @pl.when(zz != z)
-            def _():
-                y_from(k, zz * ny + y).wait_recv()
-                for copy in y_on(k, zz):
-                    copy.start()
-
-        over_z(0, visit)
+            y_from(k, zz * ny + y).wait_recv()
+            y_pass(k, zz, begin)
+
+        both_ways(d, visit)
 
     def y_use(k):
         def arrive(b):
@@ -257,27 +274,87 @@
 
         over(0, count, visit)
 
-    def y_stage(k):
-        for lag, act in ((1, y_spread), (2, y_forward), (3, y_use)):
-
-            @pl.when(has_prior & (k >= lag) & (k - lag < count))
-            def _():
-                act(k - lag)
+    def when_y(k, act):
+        @pl.when(has_prior & (k >= 0) & (k < count))
+        def _():
+            act(k)
+
+    reach = ([1], [2], list(range(3, nz)))
+
+    def s_tick(k, ds):
+        @pl.when(k < count)
+        def _():
+            for d in ds:
+                s_forward(k, d)
+
+    steps = [(min(d, 3) * LAG, d) for d in range(1, nz)]
+    last = 3 * LAG + USE
+
+    def y_tick(k, p):
+        def due(lag):
+            return (p - 2 - lag) % 3 == 0, k + (p - 2 - lag) // 3
+
+        for lag, d in steps:
+            now, m = due(lag)
+            if now:
+                when_y(m, lambda m: y_forward(m, d))
+        now, m = due(last)
+        if now:
+            when_y(m, y_use)
+        if p == 2:
+            when_y(k, y_spread)
+
+    def tick(k, p):
+        if p < 2:
+
+            @pl.when(k == 0)
+            def _():
+                s_tick(p, range(1, nz))
+
+        s_tick(k + 2, reach[p])
+        if p == 1:
+            start_own(k + 3)
+        y_tick(k, p)
 
     def keep(k):
         gathered[k, mine, :] = s_ref[:, tile(k)]
         o_ref[:, tile(k)] = d_ref[:, tile(k)]
 
     over(0, count, keep)
-    s_forward(0, 0)
+    for b in range(per):
+
+        @pl.when((b % ny == y) & (b // ny != z))
+        def _():
+            s_from(0, b).wait_recv()
+            s_pass(0, b // ny, begin)
+
+
+    even = extra == T
+    slots = max((count - k) * k for k in range(count)) if even else 0
+
+    def minus(k, j, rr):
+        return product_t(low[j, rr, :], low[j, tile(k), :])
 
     def bring(k, rr, value):
         work[rr, :] = value.astype(F32)
 
         def step(j):
-            work[rr, :] = work[rr, :] - product_t(low[j, rr, :], low[j, tile(k), :])
+            work[rr, :] = work[rr, :] - minus(k, j, rr)
 
         over(0, k, step)
+
+    def beside(k, q):
+        every = lax.max(k, 1)
+        i, j = lax.min(k + 1 + q // every, count), lax.rem(q, every)
+        to = tile(jnp.where(q < (count - k) * k, i, count + 1))
+        held = jnp.where(j == 0, 0.0, work[to, :])
+        work[to, :] = held - minus(k, j, tile(i))
+
+    def settle_rows(k, rr, value):
+        if even:
+            work[rr, :] = jnp.where(k == 0, 0.0, work[rr, :]) + value.astype(F32)
+        else:
+            bring(k, rr, value)
 
     def solve(k, rr):
         x = product_t(pair(work[rr, :]), inverse[...])
@@ -289,32 +366,32 @@
         bring(k, tile(k), gathered[k, tile(k), :])
         at = pl.multiple_of(k * T, T)
         first, second = pl.ds(at, B), pl.ds(pl.multiple_of(at + B, B), B)
-        n1 = invert(work[first, :B])
+        later = [functools.partial(beside, k, jnp.int32(q)) for q in range(slots)]
+        n1 = invert(work[first, :B], later[: slots // 2])
+        tick(k, 0)
         x21 = product_t(pair(work[second, :B]), pair(n1))
         p21 = pair(x21)
-        n2 = invert(work[second, B:] - product_t(p21, p21))
+        n2 = invert(work[second, B:] - product_t(p21, p21), later[slots // 2 :])
         m21 = product(n2, product(x21, n1))
         inverse[:B, :] = pair(jnp.concatenate([n1, jnp.zeros((B, B), F32)], 1))
         inverse[B:, :] = pair(jnp.concatenate([-m21, n2], 1))
 
-        @pl.when(k == 0)
-        def _():
-            over_z(1, lambda zz: s_forward(0, zz))
-
-        bring(k, tail, c_ref[:, tile(k)])
+        tick(k, 1)
+        settle_rows(k, tail, c_ref[:, tile(k)])
         solved[k] = solve(k, tail).astype(BF)
+
         solve(k, tile(k))
+
+        @pl.when(has_next)
+        def _():
+            y_hop(k).start()
 
         def rest(i):
             s_wait(k, i)
-            bring(k, tile(i), gathered[k, tile(i), :])
+            settle_rows(k, tile(i), gathered[k, tile(i), :])
             solve(k, tile(i))
 
         over(k + 1, count, rest)
-
-        @pl.when(has_next)
-        def _():
-            y_hop(k).start()
 
         row = me * extra + lax.broadcasted_iota(jnp.int32, (extra, T), 0)
         column = k * T + lax.broadcasted_iota(jnp.int32, (extra, T), 1)
@@ -328,38 +405,35 @@
         def _():
             f_ref[:, tile(k)] = jnp.zeros((extra, T), F32)
 
-        @pl.when(k + 1 < count)
-        def _():
-            over_z(0, lambda zz: s_forward(k + 1, zz))
-
-        y_stage(k)
+        tick(k, 2)
 
     over(0, count, chunk)
-    over(count, count + 3, y_stage)
+
+    def drain(k):
+        for p in range(3):
+            y_tick(k, p)
+
+    over(count, count + (last + 4) // 3, drain)
 
     def settle(k):
         @pl.when(s_has(k, me))
         def _():
-            for copy in s_own(k):
-                copy.wait_send()
+            s_own(k, end)
+
+        @pl.when(has_prior)
+        def _():
+            y_pass(k, z, end)
 
         def visit(zz):
             @pl.when((zz != z) & s_has(k, zz * ny + y))
             def _():
-                for copy in s_on(k, zz):
-                    copy.wait_send()
+                s_pass(k, zz, end)
 
             @pl.when((zz != z) & has_prior)
             def _():
-                for copy in y_on(k, zz):
-                    copy.wait_send()
-
-        over_z(0, visit)
-
-        @pl.when(has_prior)
-        def _():
-            for copy in y_own(k):
-                copy.wait_send()
+                y_pass(k, zz, end)
+
+        over(0, nz, visit)
 
         @pl.when(has_next)
         def _():
@@ -384,18 +458,20 @@
         scratch_shapes=[
             pltpu.VMEM((count, total, T), BF),
             pltpu.VMEM((count, total + extra, 2 * T), BF),
-            pltpu.VMEM((total + extra, T), F32),
+            pltpu.VMEM((total + extra + T, T), F32),
             pltpu.VMEM((T, 2 * T), BF),
             pltpu.VMEM((count, extra, T), BF),
             pltpu.VMEM((count, total, T), BF),
             sems((count, n)),
-            sems((count, nz - 1)),
+            sems((count, nz, 2)),
             sems((count, nz, max(ny - 1, 1))),
             sems((count,)),
             sems((count,)),
             sems((count, n)),
-            sems((count, nz - 1)),
+            sems((count, nz, 2)),
             sems((count, nz, max(ny - 1, 1))),
+            sems((2, nz - 1)),
+            sems((2, nz - 1)),
         ],
         compiler_params=pltpu.CompilerParams(
             vmem_limit_bytes=60 * 1024 * 1024, collective_id=0, has_side_effects=True

time: 232 us -> 177 us (0.76)
  Pallas kernels: 225 us -> 168 us
    pallas_call x1, Pallas kernels: 225 us -> 168 us  [local(): pl.pallas_call(functools.partial(kernel, ny), out_shape=(jax.ShapeDtypeSt...]
where the time goes in v2:
time: 177 us; the launch traced here: 174 us
  Pallas kernels  168 us (95%)
  local copies, waits for them, and re-layouts  4.61 us (3%)
    pallas_call x1, Pallas kernels, local(): pl.pallas_call(functools.partial(kernel, ny), out_shape=(jax.ShapeDtypeSt...  168 us
    unnamed x4, local copies, waits for them, and re-layouts  4.61 us

profile of v2, /device:TPU:6, one launch (start us, length us, event | category | flops | bytes accessed | tf_op | source)
XLA Modules:
  0.0 173.8 jit_solution(5858634529830495526)
XLA Ops:
  0.6 168.5 %slab_step.1 = (f32[256,2048]{1,0:T(8,128)}, f32[256,2048]{1,0:T(8,128)}) custom-call(bf16[256,2048]{1,0:T(8,128)(2,1)} %s_ref.1, bf16[256,2048]{1,0:T(8,128)(2,1)} %c_ref.1, f32[256,2048]{1,0:T(8,128)} %d_ref.1), custom_call_target="tpu_custom_call" | custom-call | tf_op jit(solution)/shard_map/slab_step/pallas_call | solution.py:453
  169.1 0.0 copy-start
  169.1 3.3 %copy.7 = f32[256,2048]{1,0:T(8,128)} copy(f32[256,2048]{1,0:T(8,128)} %get-tuple-element.4) | data formatting | bytes 4194304
  172.4 0.0 copy-done
  172.4 1.3 copy.8
Async XLA Ops:
  169.1 3.3 %copy-start = (f32[256,2048]{1,0:T(8,128)S(1)}, f32[256,2048]{1,0:T(8,128)}, u32[]{:S(2)}) copy-start(f32[256,2048]{1,0:T(8,128)} %get-tuple-element.5) | copy-start | bytes 6291460

commit v3 on v2

--- a/solution.py
+++ b/solution.py
@@ -9,7 +9,7 @@
 B = 128
 T = 2 * B
 LAG = 2
-USE = 2
+USE = 4
 BF = jnp.bfloat16
 F32 = jnp.float32
 MESH = pl.DeviceIdType.MESH
@@ -108,8 +108,8 @@
 
 def kernel(
     ny, s_ref, c_ref, d_ref, f_ref, o_ref,
-    gathered, low, work, inverse, solved, others,
-    s_recv, s_send_z, s_send_y, c_recv, c_send, y_recv, y_send_z, y_send_y, s_direct, y_direct,
+    gathered, low, work, inverse, solved, others, lent, part, part_in,
+    s_recv, s_send_z, s_send_y, c_recv, c_send, y_recv, y_send_z, y_send_y, s_direct, y_direct, l_recv, l_send_z, l_send_y, p_sem,
 ):
     extra, total = s_ref.shape
     count = total // T
@@ -126,6 +126,16 @@
     z_peers = [lax.rem(z + i, nz) * ny + y for i in range(1, nz)]
     y_peers = [(z * ny + lax.rem(y + i, ny)) for i in range(1, ny)]
     has_next, has_prior = link + 1 < links, link > 0
+    shared = 3 * count // 8
+    lends = has_next & (link % 2 == 1)
+    borrows = has_prior & (link % 2 == 0)
+
+    def hops(k):
+        return has_next & ((link % 2 == 0) | (k >= shared))
+
+    def comes(k):
+        return has_prior & ((link % 2 == 1) | (k >= shared))
+
 
     def tile(i):
         return pl.ds(pl.multiple_of(i * T, T), T)
@@ -274,8 +284,50 @@
 
         over(0, count, visit)
 
+    def l_pass(k, zz, src, act):
+        dst = lent.at[k, rows_of(zz * ny + y), :]
+        passing(src, dst, k, zz, l_send_z, l_send_y, l_recv, act, k < 0, y_direct)
+
+    def l_from(k, b):
+        at = lent.at[k, rows_of(b), :]
+        return remote(at, at, l_send_z.at[k, 0, 0], l_recv.at[k, b], blk=up)
+
+    def l_spread(k):
+        lent[k, mine, :] = solved[k]
+        l_pass(k, z, solved.at[k], begin)
+
+    def l_forward(k, d):
+        def visit(zz):
+            l_from(k, zz * ny + y).wait_recv()
+            l_pass(k, zz, lent.at[k, rows_of(zz * ny + y), :], begin)
+
+        both_ways(d, visit)
+
+    def l_use(k):
+        def arrive(b):
+            @pl.when(b % ny != y)
+            def _():
+                l_from(k, b).wait_recv()
+
+        over(0, n, arrive)
+        own = lent[k, mine, :]
+
+        def visit(j):
+            part[:, tile(j)] = part[:, tile(j)] + dot_t(own, lent[k, tile(j), :])
+
+        over(0, count, visit)
+
+    def part_hop():
+        to = lax.min(link + 1, links - 1)
+        return remote(part, part_in, p_sem.at[0], p_sem.at[1], chain=to)
+
     def when_y(k, act):
-        @pl.when(has_prior & (k >= 0) & (k < count))
+        @pl.when((k >= 0) & (k < count) & comes(k))
+        def _():
+            act(k)
+
+    def when_l(k, act):
+        @pl.when(lends & (k >= 0) & (k < shared))
         def _():
             act(k)
 
@@ -298,11 +350,18 @@
             now, m = due(lag)
             if now:
                 when_y(m, lambda m: y_forward(m, d))
+                when_l(m, lambda m: l_forward(m, d))
         now, m = due(last)
         if now:
             when_y(m, y_use)
+            when_l(m, l_use)
         if p == 2:
             when_y(k, y_spread)
+            when_l(k, l_spread)
+
+            @pl.when(lends & (k == shared + (last + 2) // 3))
+            def _():
+                part_hop().start()
 
     def tick(k, p):
         if p < 2:
@@ -319,6 +378,7 @@
     def keep(k):
         gathered[k, mine, :] = s_ref[:, tile(k)]
         o_ref[:, tile(k)] = d_ref[:, tile(k)]
+        part[:, tile(k)] = jnp.zeros((extra, T), F32)
 
     over(0, count, keep)
     for b in range(per):
@@ -382,7 +442,7 @@
 
         solve(k, tile(k))
 
-        @pl.when(has_next)
+        @pl.when(hops(k))
         def _():
             y_hop(k).start()
 
@@ -415,27 +475,40 @@
 
     over(count, count + (last + 4) // 3, drain)
 
+    @pl.when(borrows)
+    def _():
+        part_hop().wait_recv()
+
+        def fold(j):
+            o_ref[:, tile(j)] = o_ref[:, tile(j)] - part_in[:, tile(j)]
+
+        over(0, count, fold)
+
+    @pl.when(lends)
+    def _():
+        part_hop().wait_send()
+
     def settle(k):
         @pl.when(s_has(k, me))
         def _():
             s_own(k, end)
 
-        @pl.when(has_prior)
-        def _():
-            y_pass(k, z, end)
+        when_y(k, lambda m: y_pass(m, z, end))
+        when_l(k, lambda m: l_pass(m, z, solved.at[m], end))
 
         def visit(zz):
             @pl.when((zz != z) & s_has(k, zz * ny + y))
             def _():
                 s_pass(k, zz, end)
 
-            @pl.when((zz != z) & has_prior)
-            def _():
-                y_pass(k, zz, end)
+            @pl.when(zz != z)
+            def _():
+                when_y(k, lambda m: y_pass(m, zz, end))
+                when_l(k, lambda m: l_pass(m, zz, lent.at[m, rows_of(zz * ny + y), :], end))
 
         over(0, nz, visit)
 
-        @pl.when(has_next)
+        @pl.when(hops(k))
         def _():
             y_hop(k).wait_send()
 
@@ -462,6 +535,9 @@
             pltpu.VMEM((T, 2 * T), BF),
             pltpu.VMEM((count, extra, T), BF),
             pltpu.VMEM((count, total, T), BF),
+            pltpu.VMEM((count // 2, total, T), BF),
+            pltpu.VMEM((extra, total), F32),
+            pltpu.VMEM((extra, total), F32),
             sems((count, n)),
             sems((count, nz, 2)),
             sems((count, nz, max(ny - 1, 1))),
@@ -472,6 +548,10 @@
             sems((count, nz, max(ny - 1, 1))),
             sems((2, nz - 1)),
             sems((2, nz - 1)),
+            sems((count // 2, n)),
+            sems((count // 2, nz, 2)),
+            sems((count // 2, nz, max(ny - 1, 1))),
+            sems((2,)),
         ],
         compiler_params=pltpu.CompilerParams(
             vmem_limit_bytes=60 * 1024 * 1024, collective_id=0, has_side_effects=True

time: 177 us -> 174 us (0.983); the launches traced: 174 us -> 174 us
  no operation moved by 1% of the time
where the time goes in v3:
time: 174 us
  Pallas kernels  169 us (97%)
  local copies, waits for them, and re-layouts  4.61 us (3%)
    pallas_call x1, Pallas kernels, local(): pl.pallas_call(functools.partial(kernel, ny), out_shape=(jax.ShapeDtypeSt...  169 us
    unnamed x4, local copies, waits for them, and re-layouts  4.61 us

profile of v3, /device:TPU:6, one launch (start us, length us, event | category | flops | bytes accessed | tf_op | source)
XLA Modules:
  0.0 173.8 jit_solution(13885753951850063753)
XLA Ops:
  0.6 168.5 %slab_step.1 = (f32[256,2048]{1,0:T(8,128)}, f32[256,2048]{1,0:T(8,128)}) custom-call(bf16[256,2048]{1,0:T(8,128)(2,1)} %s_ref.1, bf16[256,2048]{1,0:T(8,128)(2,1)} %c_ref.1, f32[256,2048]{1,0:T(8,128)} %d_ref.1), custom_call_target="tpu_custom_call" | custom-call | tf_op jit(solution)/shard_map/slab_step/pallas_call | solution.py:526
  169.2 0.0 copy-start
  169.2 3.3 %copy.7 = f32[256,2048]{1,0:T(8,128)} copy(f32[256,2048]{1,0:T(8,128)} %get-tuple-element.4) | data formatting | bytes 4194304
  172.5 0.0 copy-done
  172.5 1.3 copy.8
Async XLA Ops:
  169.2 3.3 %copy-start = (f32[256,2048]{1,0:T(8,128)S(1)}, f32[256,2048]{1,0:T(8,128)}, u32[]{:S(2)}) copy-start(f32[256,2048]{1,0:T(8,128)} %get-tuple-element.5) | copy-start | bytes 6291460
